TPU v7x, 32 devices: a whole 2x2x4 slice. The times are simulated.
32 devices in a mesh: dp: 8 (over z, y), mp: 4 (over x, core).
Axes of the slice: x: 2, y: 2, z: 4, core: 2. Of those that a mesh axis runs over, the one named last changes fastest.
Arguments:
- tokens: bfloat16 [8, 1024, 1280], P('dp', 'mp'), may hold values from -6 to 6
- sizes: float32 [8, 1024], P('dp'), may hold values from 1 to 8
- ln1_gain: float32 [1280], replicated, may hold values from 0.25 to 1.75
- qkv_weight: bfloat16 [3, 1280, 1280], P(None, 'dp', 'mp'), may hold values from -0.15625 to 0.15625
- proj_weight: bfloat16 [1280, 1280], P('mp', 'dp'), may hold values from -0.15625 to 0.15625
- ln2_gain: float32 [1280], replicated, may hold values from 0.25 to 1.75
- fc1_weight: bfloat16 [1280, 5120], P('dp', 'mp'), may hold values from -0.15625 to 0.15625
- fc1_bias: float32 [5120], P('mp'), may hold values from -3 to 3
- fc2_weight: bfloat16 [5120, 1280], P('mp', 'dp'), may hold values from -0.078125 to 0.078125
- pair_source: int32 [8, 16], P('dp'), may hold values from 0 to 1022, as said below
- pair_target: int32 [8, 16], P('dp'), may hold values from 1 to 1023, as said below
- kept_order: int32 [8, 1008], P('dp'), may hold values from 0 to 1023, as said below
Outputs:
- merged_out: bfloat16 [8, 1008, 1280], P('dp', 'mp')
Inputs may be any that keep to these rules, and one draw needn't show every extreme that they name: `pair_source`: in each image the 16 entries are distinct even token indices. `pair_target`: odd token indices; several sources may join the same target. `kept_order`: in each image every token index that is not in pair_source appears exactly once.
All inputs are finite; a program needn't handle non-finite values.
Results may differ from a plain program's by a relative error of at most 0.017.
Values may be sent and summed in bfloat16 or wider, within the bound.
A program may use at most 64 MiB of HBM per device.

v0:
```python
import math
import jax
import jax.numpy as jnp
from jax import lax
from jax.sharding import PartitionSpec as P

D = 1280
HEADS = 16


def layer_norm(values, gain):
    center = values - jnp.mean(values, axis=-1, keepdims=True)
    spread = jnp.mean(center * center, axis=-1, keepdims=True)
    return center * lax.rsqrt(spread + 1e-06) * gain


def merge_rows(total, order_rows, source_ids, target_ids):
    kept_rows = jnp.take_along_axis(total, order_rows[:, :, None], axis=1)
    source_rows = jnp.take_along_axis(total, source_ids[:, :, None], axis=1)
    joins = (order_rows[:, :, None] == target_ids[:, None, :]).astype(jnp.float32)
    return kept_rows + jnp.einsum(
        "icr,ird->icd", joins, source_rows, precision=lax.Precision.HIGHEST
    )


def shards(
    tokens,
    sizes,
    ln1_gain,
    qkv_weight,
    proj_weight,
    ln2_gain,
    fc1_weight,
    fc1_bias,
    fc2_weight,
    pair_source,
    pair_target,
    kept_order,
):
    images, own_tokens, width = tokens.shape
    length = sizes.shape[1]
    kept_total = kept_order.shape[1]
    devices_mp = lax.axis_size("mp")
    own_start = lax.axis_index("mp") * own_tokens
    head_size = D // HEADS
    base = tokens.astype(jnp.float32)
    normed = layer_norm(base, ln1_gain).astype(jnp.bfloat16)
    whole = lax.all_gather(normed, "mp", axis=1, tiled=True)
    local_width = qkv_weight.shape[2]
    columns = whole
    projected = jnp.einsum(
        "ind,cdf->cinf",
        columns,
        lax.all_gather(qkv_weight, "dp", axis=1, tiled=True),
        preferred_element_type=jnp.float32,
    ).astype(jnp.bfloat16)
    local_heads = local_width // head_size
    shaped = projected.reshape(3, images, length, local_heads, head_size)
    queries = shaped[0]
    keys_all = shaped[1]
    values_all = shaped[2]
    size_bias = jnp.log(sizes)[:, None, None, :]
    block = min(512, length)
    outputs = []
    for begin in range(0, length, block):
        scores = (
            jnp.einsum(
                "iqhe,ikhe->ihqk",
                queries[:, begin : begin + block],
                keys_all,
                preferred_element_type=jnp.float32,
            )
            / math.sqrt(head_size)
            + size_bias
        )
        weights = jax.nn.softmax(scores, axis=-1).astype(jnp.bfloat16)
        attended_block = jnp.einsum(
            "ihqk,ikhe->iqhe", weights, values_all, preferred_element_type=jnp.float32
        )
        outputs.append(attended_block.astype(jnp.bfloat16).reshape(images, block, local_width))
    attended = jnp.concatenate(outputs, axis=1)
    branch = jnp.einsum(
        "ind,de->ine",
        attended,
        lax.all_gather(proj_weight, "dp", axis=1, tiled=True),
        preferred_element_type=jnp.float32,
    )
    weighted = sizes[:, :, None] * branch
    own_sizes = lax.dynamic_slice_in_dim(sizes, own_start, own_tokens, 1)
    own_weighted = own_sizes[:, :, None] * base
    local_total = lax.dynamic_update_slice_in_dim(
        weighted,
        lax.dynamic_slice_in_dim(weighted, own_start, own_tokens, 1) + own_weighted,
        own_start,
        1,
    )
    merged_count = kept_total // devices_mp
    own_order = lax.dynamic_slice_in_dim(
        kept_order, lax.axis_index("mp") * merged_count, merged_count, 1
    )
    scattered = lax.psum_scatter(
        jnp.transpose(
            merge_rows(local_total, kept_order, pair_source, pair_target), (1, 0, 2)
        ).astype(jnp.bfloat16),
        "mp",
        scatter_dimension=0,
        tiled=True,
    ).astype(jnp.float32)
    numerator = jnp.transpose(scattered, (1, 0, 2))
    merged_size = merge_rows(sizes[:, :, None], own_order, pair_source, pair_target)
    merged = numerator / merged_size
    normed_two = layer_norm(merged, ln2_gain).astype(jnp.bfloat16)
    gathered = lax.all_gather(normed_two, "mp", axis=1, tiled=True)
    columns = gathered
    hidden_sum = jnp.einsum(
        "imd,df->imf",
        columns,
        lax.all_gather(fc1_weight, "dp", axis=0, tiled=True),
        preferred_element_type=jnp.float32,
    )
    hidden = jax.nn.gelu(hidden_sum + fc1_bias).astype(jnp.bfloat16)
    partial_out = jnp.einsum(
        "imf,fd->imd",
        hidden,
        lax.all_gather(fc2_weight, "dp", axis=1, tiled=True),
        preferred_element_type=jnp.float32,
    )
    mlp_part = lax.psum_scatter(
        partial_out.astype(jnp.bfloat16), "mp", scatter_dimension=1, tiled=True
    ).astype(jnp.float32)
    return (merged + mlp_part).astype(jnp.bfloat16)


def solution(mesh):
    return jax.shard_map(
        shards,
        mesh=mesh,
        in_specs=(
            P("dp", "mp", None),
            P("dp", None),
            P(),
            P(None, "dp", "mp"),
            P("mp", "dp"),
            P(),
            P("dp", "mp"),
            P("mp"),
            P("mp", "dp"),
            P("dp", None),
            P("dp", None),
            P("dp", None),
        ),
        out_specs=P("dp", "mp", None),
        check_vma=False,
    )
```

profile of v0, /device:TPU:1, one launch (start us, length us, event | category | flops | bytes accessed | tf_op | source)
XLA Modules:
  0.0 317.7 jit_solution(4380768634615341311)
XLA Ops:
  6.5 0.0 all-gather.6.cloned.1.call-start
  6.6 1.3 convert_reduce_fusion
  7.9 0.0 copy-start.5
  7.9 1.4 fusion.30
  9.3 2.2 fusion.32
  11.5 0.0 all-gather.6.cloned.1.call-update
  11.6 0.0 all-gather.8.cloned.1.call-start
  11.6 0.7 all-gather.8.cloned.1.call-update
  12.3 0.0 all-gather.12.cloned.1.call-start
  12.4 0.7 all-gather.12.cloned.1.call-update
  13.0 0.0 all-gather.14.cloned.1.call-start
  13.1 0.5 all-gather.14.cloned.1.call-update
  13.6 0.0 all-gather.10.cloned.1.call-start
  13.7 0.0 copy-done.8
  13.7 0.0 copy-done
  13.7 0.0 copy-done.2
  13.8 28.3 %all_gather.20 = bf16[320,1280]{0,1:T(8,128)(2,1)S(1)} all-gather(bf16[320,160]{0,1:T(8,128)(2,1)S(1)} %copy-done.2), channel_id=1, replica_groups=mesh['dp'=8,'mp'=4] {'dp'}, dimensions={1}, use_global_device_ids=true | all-gather | bytes 921600 | tf_op jit(solution)/shard_map/all_gather | solution.py:85
  42.0 0.0 copy-done.3
  42.1 0.1 compare_select_fusion.2
  42.2 0.6 gather_fusion.3
  42.8 1.4 gather_fusion.2
  44.2 0.0 copy-done.5
  44.2 0.2 fusion.56
  44.4 53.4 %all-gather.8.cloned.1.call-done = bf16[3,1280,320]{2,1,0:T(8,128)(2,1)} async-done(((bf16[3,160,320]{2,1,0:T(8,128)(2,1)}), bf16[3,1280,320]{2,1,0:T(8,128)(2,1)}) %all-gather.8.cloned.1.call-update) | async-done | bytes 2457616 | tf_op jit(solution)/shard_map/all_gather | solution.py:54
  97.8 5.4 %convert_bitcast_fusion = bf16[3,1,1024,320]{2,3,0,1:T(8,128)(2,1)S(1)} fusion(bf16[3,1280,320]{2,1,0:T(8,128)(2,1)} %all-gather.8.cloned.1.call-done, bf16[1,1024,1280]{2,1,0:T(8,128)(2,1)} %all-gather.6.cloned.1.call-done), kind=kOutput, calls=%fused_computation.38 | convolution fusion | flops 2517565440 | bytes 7045120 | tf_op jit(solution)/shard_map/ind,cdf->cinf/dot_general | solution.py:51
  103.2 0.2 fusion.78
  103.3 4.9 %fusion.80 = (f32[4,512]{1,0:T(4,128)S(1)}, f32[4,512,1024]{2,1,0:T(8,128)}) fusion(f32[1024]{0:T(1024)S(1)} %bitcast.179, bf16[1024,4,80]{0,2,1:T(8,128)(2,1)S(1)} %bitcast.170, bf16[1,1024,4,80]{1,3,2,0:T(8,128)(2,1)S(1)} %bitcast.168), kind=kOutput, calls=%fused_computation.120 | convolution fusion | flops 343933952 | bytes 9383936 | tf_op jit(solution)/shard_map/sub | solution.py:76
  108.2 4.9 %fusion.79 = (f32[4,512]{1,0:T(4,128)S(1)}, f32[4,512,1024]{2,1,0:T(8,128)}) fusion(f32[1024]{0:T(1024)S(1)} %bitcast.180, bf16[1024,4,80]{0,2,1:T(8,128)(2,1)S(1)} %bitcast.171, bf16[1,1024,4,80]{1,3,2,0:T(8,128)(2,1)S(1)} %bitcast.169), kind=kOutput, calls=%fused_computation.119 | convolution fusion | flops 343933952 | bytes 9383936 | tf_op jit(solution)/shard_map/sub | solution.py:76
  113.0 5.1 %fusion.37 = bf16[4,80,512]{2,1,0:T(8,128)(2,1)S(1)} fusion(bf16[1024,4,80]{0,2,1:T(8,128)(2,1)S(1)} %bitcast.166, f32[4,512,1024]{2,1,0:T(8,128)} %get-tuple-element.13, f32[4,512]{1,0:T(4,128)S(1)} %get-tuple-element.12), kind=kOutput, calls=%fused_computation.55 | convolution fusion | flops 339902464 | bytes 9379840 | tf_op jit(solution)/shard_map/ihqk,ikhe->iqhe/dot_general | solution.py:77
  118.1 0.8 copy-done.9
  118.9 1.7 fusion.36
  120.6 0.0 copy-start.1
  120.6 4.0 %convolution_multiply_fusion = f32[1024,1280]{1,0:T(8,128)} fusion(bf16[320,1280]{0,1:T(8,128)(2,1)S(1)} %all_gather.20, f32[1024]{0:T(1024)S(1)} %bitcast.165, bf16[1,512,320]{1,2,0:T(8,128)(2,1)S(1)} %bitcast.173, bf16[1,512,320]{1,2,0:T(8,128)(2,1)S(1)} %bitcast.172), kind=kOutput, calls=%fused_computation.24 | convolution fusion | flops 841482240 | bytes 6721536 | tf_op jit(solution)/shard_map/ind,de->ine/dot_general | solution.py:82
  124.6 1.4 constant_dynamic-slice_fusion.2
  126.0 0.0 copy-done.1
  126.0 1.3 fusion.35
  127.3 3.1 gather_fusion.1
  130.5 9.7 %gather_fusion = f32[1008,1280]{1,0:T(8,128)} fusion(f32[1024,1280]{1,0:T(8,128)} %fusion.35, s32[1024]{0:T(1024)S(1)} %pad_clamp_fusion.2), kind=kCustom, calls=%fused_computation | custom fusion | bytes 10325952 | tf_op jit(solution)/shard_map/jit(take_along_axis)/gather | solution.py:18
  140.1 5.1 %fusion.21 = bf16[1008,1,1280]{2,0,1:T(8,128)(2,1)S(1)} fusion(f32[1008,1280]{1,0:T(8,128)} %gather_fusion, pred[1008]{0:T(1024)(128)(4,1)S(1)} %compare_and_fusion, f32[16,1280]{1,0:T(8,128)S(1)} %gather_fusion.1, pred[16]{0:T(512)(128)(4,1)S(1)} %compare_and_fusion.1, s32[1008]{0:T(1024)S(1)} %bitcast.175, s32[16]{0:T(128)S(1)} %bitcast.185), kind=kOutput, calls=%fused_computation.33 | convolution fusion | flops 251633408 | bytes 7828480 | tf_op jit(solution)/shard_map/icr,ird->icd/dot_general | solution.py:21
  145.2 0.0 copy-start.6
  145.2 0.0 copy-start.4
  145.2 27.6 %fusion = bf16[256,1280]{1,0:T(8,128)(2,1)S(1)} fusion(bf16[1008,1,1280]{2,0,1:T(8,128)(2,1)S(1)} %fusion.21), kind=kCustom, calls=%all-reduce-scatter | all-reduce-scatter fusion | flops 1310721 | bytes 3236352
  172.8 4.4 %collective-permute-start = (bf16[12,1280]{1,0:T(8,128)(2,1)S(1)}, bf16[12,1280]{1,0:T(8,128)(2,1)S(1)}, u32[]{:S(2)}, u32[]{:S(2)}) collective-permute-start(bf16[12,1280]{1,0:T(8,128)(2,1)S(1)} %slice.36), channel_id=1, source_target_pairs={{0,1},{1,2},{2,3},{4,5},{5,6},{6,7},{8,9},{9,10},{10,11},{12,13},{... | collective-permute-start | bytes 92168
  177.2 0.0 copy-done.6
  177.2 0.6 dynamic-slice.10
  178.5 0.0 collective-permute-done
  178.5 1.1 concatenate.4
  179.6 0.0 copy-start.7
  179.6 0.4 fusion.46
  180.0 0.5 multiply_reduce_fusion
  180.5 0.0 copy-done.4
  180.5 0.4 multiply_convert_fusion
  180.9 2.1 copy.14
  183.0 0.0 all-gather.10.cloned.1.call-update
  183.0 0.0 all-gather.12.cloned.1.call-done
  183.1 39.2 %all-gather.14.cloned.1.call-done = bf16[1280,1280]{0,1:T(8,128)(2,1)} async-done(((bf16[1280,160]{0,1:T(8,128)(2,1)}), bf16[1280,1280]{0,1:T(8,128)(2,1)}) %all-gather.14.cloned.1.call-update) | async-done | bytes 3276816 | tf_op jit(solution)/shard_map/all_gather | solution.py:125
  222.2 42.2 %all-gather.10.cloned.1.call-done = bf16[1,1008,1280]{2,0,1:T(2,128)(2,1)} async-done(((bf16[1,252,1280]{2,0,1:T(2,128)(2,1)}), bf16[1,1008,1280]{2,0,1:T(2,128)(2,1)}) %all-gather.10.cloned.1.call-update) | async-done | bytes 2580496 | tf_op jit(solution)/shard_map/all_gather | solution.py:113
  264.5 0.0 copy-done.7
  264.5 12.8 %fusion.20 = bf16[1,1008,1280]{2,1,0:T(8,128)(2,1)} fusion(bf16[1280,1280]{0,1:T(8,128)(2,1)} %all-gather.14.cloned.1.call-done, bf16[1280,1280]{1,0:T(8,128)(2,1)} %all-gather.12.cloned.1.call-done, bf16[1,1008,1280]{2,0,1:T(2,128)(2,1)} %all-gather.10.cloned.1.call-done, f32[1280]{0:T(1024)S(1)} %copy-done.7), kind=kOutput, calls=%fused_computation.32 | convolution fusion | flops 6620221440 | bytes 11719680 | tf_op jit(solution)/shard_map/imf,fd->imd/dot_general | solution.py:122
  277.3 26.0 %fusion.1 = bf16[256,1280]{1,0:T(8,128)(2,1)S(1)} fusion(bf16[1,1008,1280]{2,1,0:T(8,128)(2,1)} %fusion.20), kind=kCustom, calls=%all-reduce-scatter.1 | all-reduce-scatter fusion | flops 1310721 | bytes 3236352
  303.4 4.4 %collective-permute-start.1 = (bf16[12,1280]{1,0:T(8,128)(2,1)S(1)}, bf16[12,1280]{1,0:T(8,128)(2,1)S(1)}, u32[]{:S(2)}, u32[]{:S(2)}) collective-permute-start(bf16[12,1280]{1,0:T(8,128)(2,1)S(1)} %slice.37), channel_id=1, source_target_pairs={{0,1},{1,2},{2,3},{4,5},{5,6},{6,7},{8,9},{9,10},{10,11},{12,13},{... | collective-permute-start | bytes 92168
  307.8 1.1 collective-permute-done.1
  308.9 1.0 concatenate.5
  309.9 1.3 add_convert_fusion.1
  (22 shorter events, 0.1 us)
Async XLA Ops:
  6.5 7.1 %copy-start.8 = (s32[1,16]{1,0:T(1,128)S(1)}, s32[1,16]{1,0:T(1,128)}, u32[]{:S(2)}) copy-start(s32[1,16]{1,0:T(1,128)} %param.21) | copy-start | bytes 196
  6.5 7.2 %copy-start = (f32[1,1024]{1,0:T(1,128)S(1)}, f32[1,1024]{1,0:T(1,128)}, u32[]{:S(2)}) copy-start(f32[1,1024]{1,0:T(1,128)} %param.13) | copy-start | bytes 12292
  6.5 7.2 %copy-start.2 = (bf16[320,160]{0,1:T(8,128)(2,1)S(1)}, bf16[320,160]{0,1:T(8,128)(2,1)}, u32[]{:S(2)}) copy-start(bf16[320,160]{0,1:T(8,128)(2,1)} %param.16) | copy-start | bytes 307204
  6.5 35.5 %copy-start.3 = (s32[1,1008]{1,0:T(1,128)S(1)}, s32[1,1008]{1,0:T(1,128)}, u32[]{:S(2)}) copy-start(s32[1,1008]{1,0:T(1,128)} %param.23) | copy-start | bytes 12100
  6.5 37.8 %all-gather.6.cloned.1.call-start = ((), (), s32[]{:S(2)}) async-start(), calls=%async_computation | async-start | bytes 3276800 | tf_op jit(solution)/shard_map/all_gather | solution.py:48
  7.9 36.3 %copy-start.5 = (s32[1,16]{1,0:T(1,128)S(1)}, s32[1,16]{1,0:T(1,128)}, u32[]{:S(2)}) copy-start(s32[1,16]{1,0:T(1,128)} %param.22) | copy-start | bytes 196
  11.6 86.2 %all-gather.8.cloned.1.call-start = ((), (), s32[]{:S(2)}) async-start(), calls=%async_computation.1 | async-start | bytes 3317760 | tf_op jit(solution)/shard_map/all_gather | solution.py:54
  12.3 170.7 %all-gather.12.cloned.1.call-start = ((), (), s32[]{:S(2)}) async-start(), calls=%async_computation.3 | async-start | bytes 3686400 | tf_op jit(solution)/shard_map/all_gather | solution.py:118
  13.0 209.2 %all-gather.14.cloned.1.call-start = ((), (), s32[]{:S(2)}) async-start(), calls=%async_computation.4 | async-start | bytes 3686400 | tf_op jit(solution)/shard_map/all_gather | solution.py:125
  13.6 250.8 %all-gather.10.cloned.1.call-start = ((), (), s32[]{:S(2)}) async-start(), calls=%async_computation.2 | async-start | bytes 6451200 | tf_op jit(solution)/shard_map/all_gather | solution.py:113
  113.0 5.9 %copy-start.9 = (f32[4,512,1024]{2,1,0:T(8,128)S(1)}, f32[4,512,1024]{2,1,0:T(8,128)}, u32[]{:S(2)}) copy-start(f32[4,512,1024]{2,1,0:T(8,128)} %get-tuple-element.11) | copy-start | bytes 25165828
  120.6 5.4 %copy-start.1 = (bf16[1,256,1280]{2,1,0:T(8,128)(2,1)S(1)}, bf16[1,256,1280]{2,1,0:T(8,128)(2,1)}, u32[]{:S(2)}) copy-start(bf16[1,256,1280]{2,1,0:T(8,128)(2,1)} %param.12) | copy-start | bytes 1966084
  145.2 32.0 %copy-start.6 = (u32[32]{0:T(128)S(1)}, u32[32]{0:T(128)}, u32[]{:S(2)}) copy-start(u32[32]{0:T(128)} %constant.99) | copy-start | bytes 388
  145.2 35.3 %copy-start.4 = (f32[1280]{0:T(1024)S(1)}, f32[1280]{0:T(1024)}, u32[]{:S(2)}) copy-start(f32[1280]{0:T(1024)} %param.17) | copy-start | bytes 15364
  172.8 5.7 %collective-permute-start = (bf16[12,1280]{1,0:T(8,128)(2,1)S(1)}, bf16[12,1280]{1,0:T(8,128)(2,1)S(1)}, u32[]{:S(2)}, u32[]{:S(2)}) collective-permute-start(bf16[12,1280]{1,0:T(8,128)(2,1)S(1)} %slice.36), channel_id=1, source_target_pairs={{0,1},{1,2},{2,3},{4,5},{5,6},{6,7},{8,9},{9,10},{10,11},{12,13},{... | collective-permute-start | bytes 92168
  179.6 84.9 %copy-start.7 = (f32[1280]{0:T(1024)S(1)}, f32[1280]{0:T(1024)}, u32[]{:S(2)}) copy-start(f32[1280]{0:T(1024)} %param.19) | copy-start | bytes 15364
  303.4 5.5 %collective-permute-start.1 = (bf16[12,1280]{1,0:T(8,128)(2,1)S(1)}, bf16[12,1280]{1,0:T(8,128)(2,1)S(1)}, u32[]{:S(2)}, u32[]{:S(2)}) collective-permute-start(bf16[12,1280]{1,0:T(8,128)(2,1)S(1)} %slice.37), channel_id=1, source_target_pairs={{0,1},{1,2},{2,3},{4,5},{5,6},{6,7},{8,9},{9,10},{10,11},{12,13},{... | collective-permute-start | bytes 92168
Sparse Core Ops, SparseCore 0:
  11.7 27.9 all-gather.5
  41.9 55.8 all-gather.7
  100.0 59.9 all-gather.11
  162.0 60.1 all-gather.13
  223.6 40.7 all-gather.9
where the time goes:
time: 318 us
  waiting for transfers between devices  138 us (43%)
  blocking collectives  81.9 us (26%)
  matrix products  44 us (14%)
  local copies, waits for them, and re-layouts  22 us (7%)
  between operations  14.1 us (4%)
  starting transfers between devices  8.96 us (3%)
  other arithmetic  8.93 us (3%)
    unnamed x2, blocking collectives  53.6 us
    all_gather x1, waiting for transfers between devices, shards(): lax.all_gather(qkv_weight, 'dp', axis=1, tiled=True)  53.4 us
    all_gather x1, waiting for transfers between devices, shards(): gathered = lax.all_gather(normed_two, 'mp', axis=1, tiled=True)  42.2 us
    all_gather x1, waiting for transfers between devices, shards(): lax.all_gather(fc2_weight, 'dp', axis=1, tiled=True)  39.2 us
    all_gather x1, blocking collectives, shards(): lax.all_gather(proj_weight, 'dp', axis=1, tiled=True)  28.3 us
    dot_general x1, matrix products, shards(): jnp.einsum('imf,fd->imd', hidden, lax.all_gather(fc2_weight, 'dp', axis=1...  12.8 us
    gather x2, local copies, waits for them, and re-layouts, merge_rows(): kept_rows = jnp.take_along_axis(total, order_rows[:, :, None], axis=1)  11 us
    sub x2, matrix products, shards(): weights = jax.nn.softmax(scores, axis=-1).astype(jnp.bfloat16)  9.7 us
  transfers between devices with their start and end apart: 7, of which 4 were waited for; matrix products, arithmetic and copies ran while one was open for 26% of the time, Pallas kernels for 0%

commit v1 on v0

--- a/solution.py
+++ b/solution.py
@@ -6,6 +6,32 @@
 
 D = 1280
 HEADS = 16
+
+
+def ring_apply(array, axis, dim, work, out_dim):
+    size, here, rows = (lax.axis_size(axis), lax.axis_index(axis), array.shape[dim])
+    ahead = [(i, (i + 1) % size) for i in range(size)]
+    left = [(b, a) for a, b in ahead]
+    lower, upper = (lax.ppermute(array, axis, ahead), lax.ppermute(array, axis, left))
+    made = work(array, here * rows)
+    length = made.shape[out_dim]
+    result = jnp.zeros(
+        (*made.shape[:out_dim], size * length, *made.shape[out_dim + 1 :]), made.dtype
+    )
+
+    def put(result, made, owner):
+        return lax.dynamic_update_slice_in_dim(result, made, owner * length, axis=out_dim)
+
+    result = put(result, made, here)
+    for hop in range(1, size // 2 + 1):
+        below, above = ((here - hop) % size, (here + hop) % size)
+        held = (lower, upper)
+        if hop < size // 2:
+            lower, upper = (lax.ppermute(lower, axis, ahead), lax.ppermute(upper, axis, left))
+        result = put(result, work(held[0], below * rows), below)
+        if 2 * hop < size:
+            result = put(result, work(held[1], above * rows), above)
+    return result
 
 
 def layer_norm(values, gain):
@@ -79,11 +105,14 @@
         )
         outputs.append(attended_block.astype(jnp.bfloat16).reshape(images, block, local_width))
     attended = jnp.concatenate(outputs, axis=1)
-    branch = jnp.einsum(
-        "ind,de->ine",
-        attended,
-        lax.all_gather(proj_weight, "dp", axis=1, tiled=True),
-        preferred_element_type=jnp.float32,
+    branch = ring_apply(
+        proj_weight,
+        "dp",
+        1,
+        lambda part, offset: jnp.einsum(
+            "ind,de->ine", attended, part, preferred_element_type=jnp.float32
+        ),
+        2,
     )
     weighted = sizes[:, :, None] * branch
     own_sizes = lax.dynamic_slice_in_dim(sizes, own_start, own_tokens, 1)

time: 318 us -> 335 us (1.053)
  local copies, waits for them, and re-layouts: 22 us -> 74.2 us
  blocking collectives: 81.9 us -> 53.3 us
  waiting for transfers between devices: 138 us -> 110 us
  starting transfers between devices: 8.96 us -> 22.6 us
  other arithmetic: 8.93 us -> 14.6 us
    dynamic_update_slice x0 -> x8, local copies, waits for them, and re-layouts: none -> 50 us  [put(): lax.dynamic_update_slice_in_dim(result, made, owner * length, axis=out_dim)]
    all_gather x1, waiting for transfers between devices: 39.2 us -> 0.02 us  [shards(): lax.all_gather(fc2_weight, 'dp', axis=1, tiled=True)]
    all_gather x1 -> x0, blocking collectives: 28.3 us -> none  [shards(): lax.all_gather(proj_weight, 'dp', axis=1, tiled=True)]
    ppermute x0 -> x7, starting transfers between devices: none -> 13.6 us  [the longest x2 8.42 us: ring_apply(): lax.ppermute(upper, axis, left)]
    all_gather x1, waiting for transfers between devices: 0.01 us -> 5.45 us  [shards(): whole = lax.all_gather(normed, 'mp', axis=1, tiled=True)]
    ppermute x0 -> x7, waiting for transfers between devices: none -> 4.81 us  [the longest x3 4.52 us: ring_apply(): lax.ppermute(lower, axis, ahead)]
    all_gather x1, waiting for transfers between devices: 53.4 us -> 58.1 us  [shards(): lax.all_gather(qkv_weight, 'dp', axis=1, tiled=True)]
  transfers between devices with their start and end apart: 7 -> 14, of which waited for: 4 -> 7; matrix products, arithmetic and copies ran while one was open for 26% -> 41% of each run, Pallas kernels for 0% -> 0%
where the time goes in v1:
time: 335 us; the launch traced here: 333 us
  waiting for transfers between devices  110 us (33%)
  local copies, waits for them, and re-layouts  74.2 us (22%)
  blocking collectives  53.3 us (16%)
  matrix products  43.9 us (13%)
  starting transfers between devices  22.6 us (7%)
  other arithmetic  14.6 us (4%)
  between operations  14.4 us (4%)
    all_gather x1, waiting for transfers between devices, shards(): lax.all_gather(qkv_weight, 'dp', axis=1, tiled=True)  58.1 us
    unnamed x2, blocking collectives  53.3 us
    dynamic_update_slice x8, local copies, waits for them, and re-layouts, put(): lax.dynamic_update_slice_in_dim(result, made, owner * length, axis=out_dim)  50 us
    all_gather x1, waiting for transfers between devices, shards(): gathered = lax.all_gather(normed_two, 'mp', axis=1, tiled=True)  39.4 us
    dot_general x1, matrix products, shards(): jnp.einsum('imf,fd->imd', hidden, lax.all_gather(fc2_weight, 'dp', axis=1...  12.9 us
    gather x2, local copies, waits for them, and re-layouts, merge_rows(): kept_rows = jnp.take_along_axis(total, order_rows[:, :, None], axis=1)  10.9 us
    sub x2, matrix products, shards(): weights = jax.nn.softmax(scores, axis=-1).astype(jnp.bfloat16)  9.88 us
    unnamed x2, starting transfers between devices  8.77 us
  transfers between devices with their start and end apart: 14, of which 7 were waited for; matrix products, arithmetic and copies ran while one was open for 41% of the time, Pallas kernels for 0%

profile of v1, /device:TPU:1, one launch (start us, length us, event | category | flops | bytes accessed | tf_op | source)
XLA Modules:
  0.0 333.3 jit_solution(13418143411827825330)
XLA Ops:
  6.6 1.3 convert_reduce_fusion
  7.9 1.4 fusion.30
  9.3 2.2 fusion.32
  11.6 0.7 all-gather.8.cloned.1.call-update
  12.4 0.7 all-gather.12.cloned.1.call-update
  13.1 2.1 collective-permute-start
  15.2 3.1 collective-permute-start.1
  18.6 0.1 compare_select_fusion.2
  18.7 0.6 gather_fusion.3
  19.4 0.2 fusion.54
  19.6 1.4 gather_fusion.2
  21.0 0.3 collective-permute-done
  21.3 4.2 %collective-permute-start.3 = (bf16[320,160]{0,1:T(8,128)(2,1)S(1)}, bf16[320,160]{0,1:T(8,128)(2,1)S(1)}, u32[]{:S(2)}, u32[]{:S(2)}) collective-permute-start(bf16[320,160]{0,1:T(8,128)(2,1)S(1)} %collective-permute-done.1), channel_id=1, source_target_pairs={{4,0},{8,4},{12,8},{16,12},{20,16},{24,20},{28,24},{0,28},{5,1},{9... | collective-permute-start | bytes 307208 | tf_op jit(solution)/shard_map/ppermute | solution.py:30
  25.5 2.3 collective-permute-done.2
  27.8 4.2 %collective-permute-start.5 = (bf16[320,160]{0,1:T(8,128)(2,1)S(1)}, bf16[320,160]{0,1:T(8,128)(2,1)S(1)}, u32[]{:S(2)}, u32[]{:S(2)}) collective-permute-start(bf16[320,160]{0,1:T(8,128)(2,1)S(1)} %collective-permute-done.3), channel_id=1, source_target_pairs={{4,0},{8,4},{12,8},{16,12},{20,16},{24,20},{28,24},{0,28},{5,1},{9... | collective-permute-start | bytes 307208 | tf_op jit(solution)/shard_map/ppermute | solution.py:30
  32.0 2.2 collective-permute-done.4
  34.3 5.5 %all-gather.6.cloned.1.call-done = bf16[1,1024,1280]{2,1,0:T(8,128)(2,1)} async-done(((bf16[1,256,1280]{2,1,0:T(8,128)(2,1)}), bf16[1,1024,1280]{2,1,0:T(8,128)(2,1)}) %all-gather.6.cloned.1.call-update) | async-done | bytes 2621456 | tf_op jit(solution)/shard_map/all_gather | solution.py:74
  39.7 58.1 %all-gather.8.cloned.1.call-done = bf16[3,1280,320]{2,1,0:T(8,128)(2,1)} async-done(((bf16[3,160,320]{2,1,0:T(8,128)(2,1)}), bf16[3,1280,320]{2,1,0:T(8,128)(2,1)}) %all-gather.8.cloned.1.call-update) | async-done | bytes 2457616 | tf_op jit(solution)/shard_map/all_gather | solution.py:80
  97.8 5.4 %convert_bitcast_fusion = bf16[3,1,1024,320]{2,3,0,1:T(8,128)(2,1)S(1)} fusion(bf16[3,1280,320]{2,1,0:T(8,128)(2,1)} %all-gather.8.cloned.1.call-done, bf16[1,1024,1280]{2,1,0:T(8,128)(2,1)} %all-gather.6.cloned.1.call-done), kind=kOutput, calls=%fused_computation.38 | convolution fusion | flops 2517565440 | bytes 7045120 | tf_op jit(solution)/shard_map/ind,cdf->cinf/dot_general | solution.py:77
  103.2 0.2 fusion.75
  103.3 5.0 %fusion.77 = (f32[4,512]{1,0:T(4,128)S(1)}, f32[4,512,1024]{2,1,0:T(8,128)}) fusion(f32[1024]{0:T(1024)S(1)} %bitcast.224, bf16[1024,4,80]{0,2,1:T(8,128)(2,1)S(1)} %bitcast.217, bf16[1,1024,4,80]{1,3,2,0:T(8,128)(2,1)S(1)} %bitcast.215), kind=kOutput, calls=%fused_computation.124 | convolution fusion | flops 343933952 | bytes 9383936 | tf_op jit(solution)/shard_map/sub | solution.py:102
  108.3 4.9 %fusion.76 = (f32[4,512]{1,0:T(4,128)S(1)}, f32[4,512,1024]{2,1,0:T(8,128)}) fusion(f32[1024]{0:T(1024)S(1)} %bitcast.225, bf16[1024,4,80]{0,2,1:T(8,128)(2,1)S(1)} %bitcast.218, bf16[1,1024,4,80]{1,3,2,0:T(8,128)(2,1)S(1)} %bitcast.216), kind=kOutput, calls=%fused_computation.123 | convolution fusion | flops 343933952 | bytes 9383936 | tf_op jit(solution)/shard_map/sub | solution.py:102
  113.2 5.1 %fusion.37 = bf16[4,80,512]{2,1,0:T(8,128)(2,1)S(1)} fusion(bf16[1024,4,80]{0,2,1:T(8,128)(2,1)S(1)} %bitcast.213, f32[4,512,1024]{2,1,0:T(8,128)} %get-tuple-element.13, f32[4,512]{1,0:T(4,128)S(1)} %get-tuple-element.12), kind=kOutput, calls=%fused_computation.63 | convolution fusion | flops 339902464 | bytes 9379840 | tf_op jit(solution)/shard_map/ihqk,ikhe->iqhe/dot_general | solution.py:103
  118.3 0.8 copy-done.10
  119.1 1.7 fusion.36
  120.8 0.5 convolution_bitcast_fusion.7
  121.3 2.6 broadcast_in_dim.68
  123.9 5.9 %dynamic_update_slice.27 = f32[1,1024,1280]{2,1,0:T(8,128)} dynamic-update-slice(f32[1,1024,1280]{2,1,0:T(8,128)} %broadcast_in_dim.68, f32[1,1024,160]{2,1,0:T(8,128)S(1)} %convolution_bitcast_fusion.7, s32[]{:T(128)} %constant.122.clone.1, s32[]{:T(128)} %constant.122.clone.1, s32[]{:T(128)S(6)} %select_n.205) | dynamic-update-slice | bytes 1310724 | tf_op jit(solution)/shard_map/dynamic_update_slice | solution.py:23
  129.8 0.5 convolution_bitcast_fusion.6
  130.2 5.9 %dynamic_update_slice.28 = f32[1,1024,1280]{2,1,0:T(8,128)} dynamic-update-slice(f32[1,1024,1280]{2,1,0:T(8,128)} %dynamic_update_slice.27, f32[1,1024,160]{2,1,0:T(8,128)S(1)} %convolution_bitcast_fusion.6, s32[]{:T(128)} %constant.122.clone.1, s32[]{:T(128)} %constant.122.clone.1, s32[]{:T(128)S(6)} %select_n.207) | dynamic-update-slice | bytes 1310724 | tf_op jit(solution)/shard_map/dynamic_update_slice | solution.py:23
  136.1 0.5 convolution_bitcast_fusion.5
  136.6 6.5 %dynamic_update_slice.29 = f32[1,1024,1280]{2,1,0:T(8,128)} dynamic-update-slice(f32[1,1024,1280]{2,1,0:T(8,128)} %dynamic_update_slice.28, f32[1,1024,160]{2,1,0:T(8,128)S(1)} %convolution_bitcast_fusion.5, s32[]{:T(128)} %constant.122.clone.1, s32[]{:T(128)} %constant.122.clone.1, s32[]{:T(128)S(6)} %select_n.209) | dynamic-update-slice | bytes 1310724 | tf_op jit(solution)/shard_map/dynamic_update_slice | solution.py:23
  143.1 0.5 convolution_bitcast_fusion.4
  143.6 6.3 %dynamic_update_slice.30 = f32[1,1024,1280]{2,1,0:T(8,128)} dynamic-update-slice(f32[1,1024,1280]{2,1,0:T(8,128)} %dynamic_update_slice.29, f32[1,1024,160]{2,1,0:T(8,128)S(1)} %convolution_bitcast_fusion.4, s32[]{:T(128)} %constant.122.clone.1, s32[]{:T(128)} %constant.122.clone.1, s32[]{:T(128)S(6)} %select_n.211) | dynamic-update-slice | bytes 1310724 | tf_op jit(solution)/shard_map/dynamic_update_slice | solution.py:23
  149.9 0.5 convolution_bitcast_fusion.3
  150.4 6.5 %dynamic_update_slice.31 = f32[1,1024,1280]{2,1,0:T(8,128)} dynamic-update-slice(f32[1,1024,1280]{2,1,0:T(8,128)} %dynamic_update_slice.30, f32[1,1024,160]{2,1,0:T(8,128)S(1)} %convolution_bitcast_fusion.3, s32[]{:T(128)} %constant.122.clone.1, s32[]{:T(128)} %constant.122.clone.1, s32[]{:T(128)S(6)} %select_n.213) | dynamic-update-slice | bytes 1310724 | tf_op jit(solution)/shard_map/dynamic_update_slice | solution.py:23
  156.9 0.5 convolution_bitcast_fusion.2
  157.4 6.5 %dynamic_update_slice.32 = f32[1,1024,1280]{2,1,0:T(8,128)} dynamic-update-slice(f32[1,1024,1280]{2,1,0:T(8,128)} %dynamic_update_slice.31, f32[1,1024,160]{2,1,0:T(8,128)S(1)} %convolution_bitcast_fusion.2, s32[]{:T(128)} %constant.122.clone.1, s32[]{:T(128)} %constant.122.clone.1, s32[]{:T(128)S(6)} %select_n.215) | dynamic-update-slice | bytes 1310724 | tf_op jit(solution)/shard_map/dynamic_update_slice | solution.py:23
  163.9 0.5 convolution_bitcast_fusion.1
  164.4 6.5 %dynamic_update_slice.33 = f32[1,1024,1280]{2,1,0:T(8,128)} dynamic-update-slice(f32[1,1024,1280]{2,1,0:T(8,128)} %dynamic_update_slice.32, f32[1,1024,160]{2,1,0:T(8,128)S(1)} %convolution_bitcast_fusion.1, s32[]{:T(128)} %constant.122.clone.1, s32[]{:T(128)} %constant.122.clone.1, s32[]{:T(128)S(6)} %select_n.217) | dynamic-update-slice | bytes 1310724 | tf_op jit(solution)/shard_map/dynamic_update_slice | solution.py:23
  170.8 0.5 convolution_bitcast_fusion
  171.3 6.0 %dynamic_update_slice.34 = f32[1,1024,1280]{2,1,0:T(8,128)} dynamic-update-slice(f32[1,1024,1280]{2,1,0:T(8,128)} %dynamic_update_slice.33, f32[1,1024,160]{2,1,0:T(8,128)S(1)} %convolution_bitcast_fusion, s32[]{:T(128)} %constant.122.clone.1, s32[]{:T(128)} %constant.122.clone.1, s32[]{:T(128)S(6)} %select_n.219) | dynamic-update-slice | bytes 1310724 | tf_op jit(solution)/shard_map/dynamic_update_slice | solution.py:23
  177.3 3.1 broadcast_multiply_fusion
  180.4 1.0 copy-done.1
  181.4 2.7 fusion.96
  184.1 1.3 fusion.35
  185.3 3.1 gather_fusion.1
  188.5 9.6 %gather_fusion = f32[1008,1280]{1,0:T(8,128)} fusion(f32[1024,1280]{1,0:T(8,128)} %fusion.35, s32[1024]{0:T(1024)S(1)} %pad_clamp_fusion.2), kind=kCustom, calls=%fused_computation | custom fusion | bytes 10325952 | tf_op jit(solution)/shard_map/jit(take_along_axis)/gather | solution.py:44
  198.0 5.1 %fusion.21 = bf16[1008,1,1280]{2,0,1:T(8,128)(2,1)S(1)} fusion(f32[1008,1280]{1,0:T(8,128)} %gather_fusion, pred[1008]{0:T(1024)(128)(4,1)S(1)} %compare_and_fusion, f32[16,1280]{1,0:T(8,128)S(1)} %gather_fusion.1, pred[16]{0:T(512)(128)(4,1)S(1)} %compare_and_fusion.1, s32[1008]{0:T(1024)S(1)} %bitcast.220, s32[16]{0:T(128)S(1)} %bitcast.230), kind=kOutput, calls=%fused_computation.32 | convolution fusion | flops 251633408 | bytes 7828480 | tf_op jit(solution)/shard_map/icr,ird->icd/dot_general | solution.py:47
  203.1 27.3 %fusion = bf16[256,1280]{1,0:T(8,128)(2,1)S(1)} fusion(bf16[1008,1,1280]{2,0,1:T(8,128)(2,1)S(1)} %fusion.21), kind=kCustom, calls=%all-reduce-scatter | all-reduce-scatter fusion | flops 1310721 | bytes 3236352
  230.4 4.4 %collective-permute-start.7 = (bf16[12,1280]{1,0:T(8,128)(2,1)S(1)}, bf16[12,1280]{1,0:T(8,128)(2,1)S(1)}, u32[]{:S(2)}, u32[]{:S(2)}) collective-permute-start(bf16[12,1280]{1,0:T(8,128)(2,1)S(1)} %slice.36), channel_id=1, source_target_pairs={{0,1},{1,2},{2,3},{4,5},{5,6},{6,7},{8,9},{9,10},{10,11},{12,13},{... | collective-permute-start | bytes 92168
  234.8 0.6 dynamic-slice.6
  236.1 1.1 concatenate.4
  237.2 0.4 fusion.44
  237.6 0.5 multiply_reduce_fusion
  238.1 0.4 multiply_convert_fusion
  238.5 2.1 copy.46
  240.7 39.4 %all-gather.10.cloned.1.call-done = bf16[1,1008,1280]{2,0,1:T(2,128)(2,1)} async-done(((bf16[1,252,1280]{2,0,1:T(2,128)(2,1)}), bf16[1,1008,1280]{2,0,1:T(2,128)(2,1)}) %all-gather.10.cloned.1.call-update) | async-done | bytes 2580496 | tf_op jit(solution)/shard_map/all_gather | solution.py:142
  280.1 12.9 %fusion.20 = bf16[1,1008,1280]{2,1,0:T(8,128)(2,1)} fusion(bf16[1280,1280]{0,1:T(8,128)(2,1)} %all-gather.14.cloned.1.call-done, bf16[1280,1280]{1,0:T(8,128)(2,1)} %all-gather.12.cloned.1.call-done, bf16[1,1008,1280]{2,0,1:T(2,128)(2,1)} %all-gather.10.cloned.1.call-done, f32[1280]{0:T(1024)S(1)} %copy-done.8), kind=kOutput, calls=%fused_computation.31 | convolution fusion | flops 6620221440 | bytes 11719680 | tf_op jit(solution)/shard_map/imf,fd->imd/dot_general | solution.py:151
  292.9 26.0 %fusion.1 = bf16[256,1280]{1,0:T(8,128)(2,1)S(1)} fusion(bf16[1,1008,1280]{2,1,0:T(8,128)(2,1)} %fusion.20), kind=kCustom, calls=%all-reduce-scatter.1 | all-reduce-scatter fusion | flops 1310721 | bytes 3236352
  319.0 4.4 %collective-permute-start.8 = (bf16[12,1280]{1,0:T(8,128)(2,1)S(1)}, bf16[12,1280]{1,0:T(8,128)(2,1)S(1)}, u32[]{:S(2)}, u32[]{:S(2)}) collective-permute-start(bf16[12,1280]{1,0:T(8,128)(2,1)S(1)} %slice.37), channel_id=1, source_target_pairs={{0,1},{1,2},{2,3},{4,5},{5,6},{6,7},{8,9},{9,10},{10,11},{12,13},{... | collective-permute-start | bytes 92168
  323.4 1.1 collective-permute-done.8
  324.5 1.0 concatenate.5
  325.5 1.3 add_convert_fusion.1
  (54 shorter events, 0.5 us)
Async XLA Ops:
  6.5 6.6 %copy-start.3 = (bf16[320,160]{0,1:T(8,128)(2,1)S(1)}, bf16[320,160]{0,1:T(8,128)(2,1)}, u32[]{:S(2)}) copy-start(bf16[320,160]{0,1:T(8,128)(2,1)} %param.16) | copy-start | bytes 307204
  6.5 12.0 %copy-start.9 = (s32[1,16]{1,0:T(1,128)S(1)}, s32[1,16]{1,0:T(1,128)}, u32[]{:S(2)}) copy-start(s32[1,16]{1,0:T(1,128)} %param.21) | copy-start | bytes 196
  6.5 12.0 %copy-start = (f32[1,1024]{1,0:T(1,128)S(1)}, f32[1,1024]{1,0:T(1,128)}, u32[]{:S(2)}) copy-start(f32[1,1024]{1,0:T(1,128)} %param.13) | copy-start | bytes 12292
  6.5 12.0 %copy-start.4 = (s32[1,1008]{1,0:T(1,128)S(1)}, s32[1,1008]{1,0:T(1,128)}, u32[]{:S(2)}) copy-start(s32[1,1008]{1,0:T(1,128)} %param.23) | copy-start | bytes 12100
  6.5 12.8 %copy-start.6 = (s32[1,16]{1,0:T(1,128)S(1)}, s32[1,16]{1,0:T(1,128)}, u32[]{:S(2)}) copy-start(s32[1,16]{1,0:T(1,128)} %param.22) | copy-start | bytes 196
  6.5 33.2 %all-gather.6.cloned.1.call-start = ((), (), s32[]{:S(2)}) async-start(), calls=%async_computation | async-start | bytes 3276800 | tf_op jit(solution)/shard_map/all_gather | solution.py:74
  11.6 86.2 %all-gather.8.cloned.1.call-start = ((), (), s32[]{:S(2)}) async-start(), calls=%async_computation.1 | async-start | bytes 3317760 | tf_op jit(solution)/shard_map/all_gather | solution.py:80
  12.3 228.4 %all-gather.12.cloned.1.call-start = ((), (), s32[]{:S(2)}) async-start(), calls=%async_computation.3 | async-start | bytes 3686400 | tf_op jit(solution)/shard_map/all_gather | solution.py:147
  13.1 227.7 %all-gather.14.cloned.1.call-start = ((), (), s32[]{:S(2)}) async-start(), calls=%async_computation.4 | async-start | bytes 3686400 | tf_op jit(solution)/shard_map/all_gather | solution.py:154
  13.1 8.2 %collective-permute-start = (bf16[320,160]{0,1:T(8,128)(2,1)S(1)}, bf16[320,160]{0,1:T(8,128)(2,1)S(1)}, u32[]{:S(2)}, u32[]{:S(2)}) collective-permute-start(bf16[320,160]{0,1:T(8,128)(2,1)S(1)} %copy-done.3), channel_id=1, source_target_pairs={{0,4},{4,8},{8,12},{12,16},{16,20},{20,24},{24,28},{28,0},{1,5},{5... | collective-permute-start | bytes 307208 | tf_op jit(solution)/shard_map/ppermute | solution.py:15
  15.2 6.1 %collective-permute-start.1 = (bf16[320,160]{0,1:T(8,128)(2,1)S(1)}, bf16[320,160]{0,1:T(8,128)(2,1)S(1)}, u32[]{:S(2)}, u32[]{:S(2)}) collective-permute-start(bf16[320,160]{0,1:T(8,128)(2,1)S(1)} %copy-done.3), channel_id=1, source_target_pairs={{4,0},{8,4},{12,8},{16,12},{20,16},{24,20},{28,24},{0,28},{5,1},{9... | collective-permute-start | bytes 307208 | tf_op jit(solution)/shard_map/ppermute | solution.py:15
  18.3 261.7 %all-gather.10.cloned.1.call-start = ((), (), s32[]{:S(2)}) async-start(), calls=%async_computation.2 | async-start | bytes 6451200 | tf_op jit(solution)/shard_map/all_gather | solution.py:142
  21.3 6.5 %collective-permute-start.2 = (bf16[320,160]{0,1:T(8,128)(2,1)S(1)}, bf16[320,160]{0,1:T(8,128)(2,1)S(1)}, u32[]{:S(2)}, u32[]{:S(2)}) collective-permute-start(bf16[320,160]{0,1:T(8,128)(2,1)S(1)} %collective-permute-done), channel_id=1, source_target_pairs={{0,4},{4,8},{8,12},{12,16},{16,20},{20,24},{24,28},{28,0},{1,5},{5... | collective-permute-start | bytes 307208 | tf_op jit(solution)/shard_map/ppermute | solution.py:30
  21.3 6.5 %collective-permute-start.3 = (bf16[320,160]{0,1:T(8,128)(2,1)S(1)}, bf16[320,160]{0,1:T(8,128)(2,1)S(1)}, u32[]{:S(2)}, u32[]{:S(2)}) collective-permute-start(bf16[320,160]{0,1:T(8,128)(2,1)S(1)} %collective-permute-done.1), channel_id=1, source_target_pairs={{4,0},{8,4},{12,8},{16,12},{20,16},{24,20},{28,24},{0,28},{5,1},{9... | collective-permute-start | bytes 307208 | tf_op jit(solution)/shard_map/ppermute | solution.py:30
  27.8 6.4 %collective-permute-start.4 = (bf16[320,160]{0,1:T(8,128)(2,1)S(1)}, bf16[320,160]{0,1:T(8,128)(2,1)S(1)}, u32[]{:S(2)}, u32[]{:S(2)}) collective-permute-start(bf16[320,160]{0,1:T(8,128)(2,1)S(1)} %collective-permute-done.2), channel_id=1, source_target_pairs={{0,4},{4,8},{8,12},{12,16},{16,20},{20,24},{24,28},{28,0},{1,5},{5... | collective-permute-start | bytes 307208 | tf_op jit(solution)/shard_map/ppermute | solution.py:30
  27.8 136.1 %collective-permute-start.5 = (bf16[320,160]{0,1:T(8,128)(2,1)S(1)}, bf16[320,160]{0,1:T(8,128)(2,1)S(1)}, u32[]{:S(2)}, u32[]{:S(2)}) collective-permute-start(bf16[320,160]{0,1:T(8,128)(2,1)S(1)} %collective-permute-done.3), channel_id=1, source_target_pairs={{4,0},{8,4},{12,8},{16,12},{20,16},{24,20},{28,24},{0,28},{5,1},{9... | collective-permute-start | bytes 307208 | tf_op jit(solution)/shard_map/ppermute | solution.py:30
  34.3 136.6 %collective-permute-start.6 = (bf16[320,160]{0,1:T(8,128)(2,1)S(1)}, bf16[320,160]{0,1:T(8,128)(2,1)S(1)}, u32[]{:S(2)}, u32[]{:S(2)}) collective-permute-start(bf16[320,160]{0,1:T(8,128)(2,1)S(1)} %collective-permute-done.4), channel_id=1, source_target_pairs={{0,4},{4,8},{8,12},{12,16},{16,20},{20,24},{24,28},{28,0},{1,5},{5... | collective-permute-start | bytes 307208 | tf_op jit(solution)/shard_map/ppermute | solution.py:30
  113.2 5.8 %copy-start.10 = (f32[4,512,1024]{2,1,0:T(8,128)S(1)}, f32[4,512,1024]{2,1,0:T(8,128)}, u32[]{:S(2)}) copy-start(f32[4,512,1024]{2,1,0:T(8,128)} %get-tuple-element.11) | copy-start | bytes 25165828
  177.3 4.1 %copy-start.1 = (f32[1,1024,1280]{2,1,0:T(8,128)S(1)}, f32[1,1024,1280]{2,1,0:T(8,128)}, u32[]{:S(2)}) copy-start(f32[1,1024,1280]{2,1,0:T(8,128)} %dynamic_update_slice.34) | copy-start | bytes 15728644
  181.4 2.7 copy-start.2
  203.1 31.7 %copy-start.7 = (u32[32]{0:T(128)S(1)}, u32[32]{0:T(128)}, u32[]{:S(2)}) copy-start(u32[32]{0:T(128)} %constant.160) | copy-start | bytes 388
  203.1 35.0 %copy-start.5 = (f32[1280]{0:T(1024)S(1)}, f32[1280]{0:T(1024)}, u32[]{:S(2)}) copy-start(f32[1280]{0:T(1024)} %param.17) | copy-start | bytes 15364
  230.4 5.7 %collective-permute-start.7 = (bf16[12,1280]{1,0:T(8,128)(2,1)S(1)}, bf16[12,1280]{1,0:T(8,128)(2,1)S(1)}, u32[]{:S(2)}, u32[]{:S(2)}) collective-permute-start(bf16[12,1280]{1,0:T(8,128)(2,1)S(1)} %slice.36), channel_id=1, source_target_pairs={{0,1},{1,2},{2,3},{4,5},{5,6},{6,7},{8,9},{9,10},{10,11},{12,13},{... | collective-permute-start | bytes 92168
  237.2 42.9 %copy-start.8 = (f32[1280]{0:T(1024)S(1)}, f32[1280]{0:T(1024)}, u32[]{:S(2)}) copy-start(f32[1280]{0:T(1024)} %param.19) | copy-start | bytes 15364
  319.0 5.5 %collective-permute-start.8 = (bf16[12,1280]{1,0:T(8,128)(2,1)S(1)}, bf16[12,1280]{1,0:T(8,128)(2,1)S(1)}, u32[]{:S(2)}, u32[]{:S(2)}) collective-permute-start(bf16[12,1280]{1,0:T(8,128)(2,1)S(1)} %slice.37), channel_id=1, source_target_pairs={{0,1},{1,2},{2,3},{4,5},{5,6},{6,7},{8,9},{9,10},{10,11},{12,13},{... | collective-permute-start | bytes 92168
Sparse Core Ops, SparseCore 0:
  11.7 27.9 all-gather.5
  41.9 55.8 all-gather.7
  100.0 60.0 all-gather.11
  162.1 60.0 all-gather.13
  240.8 39.2 all-gather.9
